TPU v7x, 256 devices: a whole 4x4x8 slice. The times are simulated.
256 devices in a mesh: rep: 16 (over y_lo, x, core), blk: 16 (over z, y_hi).
Axes of the slice: x: 4, y: 4 (y_hi: 2, y_lo: 2; y = y_hi * 2 + y_lo), z: 8, core: 2. Of those that a mesh axis runs over, the one named last changes fastest.
Arguments:
- features: bfloat16 [2, 4096, 2048], P(None, 'rep'), may hold values from -0.125 to 0.125
- grad_act: bfloat16 [2, 4096, 24576], P(None, 'rep', 'blk'), may hold values from -2.5 to 2.5
- weights: bfloat16 [2048, 24576], P(None, 'blk'), may hold values from -6 to 6
- owner_slot: int32 [16, 48], P('blk'), may hold values from 0 to 47, each once within a row
- factors: float32 [16, 48, 2, 256, 256], P('blk', 'rep'), may hold values from -100 to 250, as said below
- roots: bfloat16 [16, 48, 2, 256, 256], P('blk', 'rep'), may hold values from -1 to 2, as said below
- helper_list: int32 [2, 16, 4], replicated, may hold values from 0 to 95, as said below
Outputs:
- weights_out: bfloat16 [16, 48, 256, 256], P('blk', 'rep')
- roots_out: bfloat16 [16, 48, 2, 256, 256], P('blk', 'rep')
Inputs may be any that keep to these rules, and one draw needn't show every extreme that they name: `owner_slot`: each row is a permutation of the slots of one group; slot s belongs to index s // 3 of rep. `factors`: symmetric positive definite. `roots`: Symmetric. `helper_list`: In a step every helper has exactly 4 ids, no id appears twice, and no helper has two ids of one group; a group has at most min(6, 16) of its ids in a step.
All inputs are finite; a program needn't handle non-finite values.
Results may differ from a plain program's by a relative error of at most 0.0085.
Values may be sent and summed in bfloat16 or wider, within the bound.
A program may use at most 128 MiB of HBM per device.

v0:
```python
import jax
import jax.numpy as jnp
from jax import lax
from jax.sharding import PartitionSpec as P

NEWTON = 3
RIDGE = 0.001
NORM_EPS = 1e-06
DECAY = 0.95
STEP_SIZE = 0.5


def exact_dot(first, second):
    return jnp.einsum("...ij,...jk->...ik", first, second)


def inverse_root(matrices):
    identity = jnp.eye(matrices.shape[-1], dtype=jnp.float32)
    ridged = matrices + RIDGE * identity
    norm_scale = jnp.sqrt(jnp.sum(ridged * ridged, axis=(-2, -1), keepdims=True) + NORM_EPS)
    current = ridged / norm_scale
    result = identity
    for newton_turn in range(NEWTON):
        factor = (5.0 * identity - current) / 4.0
        if newton_turn == 0:
            result = factor * norm_scale ** (-0.25)
        else:
            result = exact_dot(result, factor)
        if newton_turn + 1 < NEWTON:
            square = exact_dot(factor, factor)
            current = exact_dot(exact_dot(square, square), current)
    return result.astype(jnp.bfloat16)


def silu_slope(value):
    sigmoid = jax.nn.sigmoid(value)
    return sigmoid * (1.0 + value * (1.0 - sigmoid))


def body(features, grad_act, weights, owner_slot, factors, roots, helper_list):
    block_size = factors.shape[-1]
    owned = factors.shape[1]
    per_owner = 2 * owned
    slot_count = owner_slot.shape[1]
    token_count = features.shape[1]
    row_blocks = features.shape[2] // block_size
    col_blocks = grad_act.shape[2] // block_size
    rep_index = lax.axis_index("rep")
    blk_index = lax.axis_index("blk")
    slot_ids = jnp.arange(slot_count, dtype=jnp.int32)
    placing = owner_slot[0][None, :] == slot_ids[:, None]
    block_at = jnp.sum(jnp.where(placing, slot_ids[None, :], 0), axis=1)
    row_at = block_at // col_blocks
    column_pick = (
        (block_at % col_blocks)[:, None] == jnp.arange(col_blocks, dtype=jnp.int32)[None, :]
    ).astype(jnp.float32)
    mine = lax.dynamic_slice_in_dim(block_at, rep_index * owned, owned)
    grid = weights.reshape(row_blocks, block_size, col_blocks, block_size)
    own_weight = grid[mine // col_blocks, :, mine % col_blocks, :]
    current_factors = factors[0]
    current_roots = roots[0]
    owner_ids = blk_index * per_owner + jnp.arange(per_owner, dtype=jnp.int32)
    for step_index in range(features.shape[0]):
        features_now = features[step_index]
        feature_blocks = features_now.reshape(token_count, row_blocks, block_size)
        if step_index == 0:
            gate_value = jnp.dot(features_now, weights, preferred_element_type=jnp.float32)
        else:
            chosen = jnp.take(feature_blocks, row_at, axis=1)
            products = jnp.einsum(
                "tsa,sab->tsb",
                chosen,
                lax.all_gather(own_weight, "rep", axis=0, tiled=True),
                preferred_element_type=jnp.float32,
            )
            gate_value = jnp.einsum("tsb,sj->tjb", products, column_pick)
            gate_value = gate_value.reshape(token_count, col_blocks * block_size)
        dgate = (grad_act[step_index].astype(jnp.float32) * silu_slope(gate_value)).astype(
            jnp.bfloat16
        )
        dgate_blocks = dgate.reshape(token_count, col_blocks, block_size)
        left_rows = jnp.take(feature_blocks, block_at // col_blocks, axis=1)
        right_cols = jnp.take(dgate_blocks, block_at % col_blocks, axis=1)
        grads = lax.psum_scatter(
            jnp.einsum(
                "tsa,tsb->sab", left_rows, right_cols, preferred_element_type=jnp.float32
            ).astype(jnp.bfloat16),
            "rep",
            scatter_dimension=0,
            tiled=True,
        ).astype(jnp.float32)
        grads_low = grads.astype(jnp.bfloat16)
        left_side = jnp.einsum(
            "kij,kjl->kil", current_roots[:, 0], grads_low, preferred_element_type=jnp.float32
        ).astype(jnp.bfloat16)
        shaped = jnp.einsum(
            "kij,kjl->kil", left_side, current_roots[:, 1], preferred_element_type=jnp.float32
        )
        grad_norm = jnp.sqrt(jnp.sum(grads * grads, axis=(-2, -1), keepdims=True) + NORM_EPS)
        shaped_norm = jnp.sqrt(jnp.sum(shaped * shaped, axis=(-2, -1), keepdims=True) + NORM_EPS)
        stored_weight = lax.optimization_barrier(own_weight).astype(jnp.float32)
        own_weight = (stored_weight - STEP_SIZE * (grad_norm / shaped_norm) * shaped).astype(
            jnp.bfloat16
        )
        left_stat = exact_dot(grads, jnp.swapaxes(grads, -1, -2))
        right_stat = exact_dot(jnp.swapaxes(grads, -1, -2), grads)
        current_factors = DECAY * current_factors + (1.0 - DECAY) * jnp.stack(
            [left_stat, right_stat], axis=1
        )
        flat_factors = current_factors.reshape(per_owner, block_size, block_size)
        listing = helper_list[step_index]
        matches = listing[:, :, None] == owner_ids[None, None, :]
        sending = jnp.any(matches, axis=1).astype(jnp.float32)
        refreshed = jnp.sum(sending, axis=0)
        computed = inverse_root(flat_factors)
        previous = current_roots.reshape(per_owner, block_size, block_size)
        current_roots = jnp.where(refreshed[:, None, None] > 0.5, computed, previous).reshape(
            owned, 2, block_size, block_size
        )
    return (own_weight[None], current_roots[None])


def solution(mesh):
    return jax.shard_map(
        body,
        mesh=mesh,
        in_specs=(
            P(None, "rep", None),
            P(None, "rep", "blk"),
            P(None, "blk"),
            P("blk", None),
            P("blk", "rep", None, None, None),
            P("blk", "rep", None, None, None),
            P(),
        ),
        out_specs=(P("blk", "rep", None, None), P("blk", "rep", None, None, None)),
        check_vma=False,
    )
```

profile of v0, /device:TPU:32, one launch (start us, length us, event | category | flops | bytes accessed | tf_op | source)
XLA Modules:
  0.0 321.1 jit_solution(12098752500672347873)
XLA Ops:
  8.0 1.7 fusion.168
  10.8 5.4 %fusion.46 = bf16[256,1536]{1,0:T(8,128)(2,1)S(1)} fusion(bf16[2048,1536]{1,0:T(8,128)(2,1)} %param.13, bf16[2,256,1536]{2,1,0:T(8,128)(2,1)} %param.12, bf16[2,256,2048]{2,1,0:T(8,128)(2,1)} %param.11), kind=kOutput, calls=%fused_computation.43 | convolution fusion | flops 1614544896 | bytes 8912896 | tf_op jit(solution)/shard_map/dot_general | solution.py:67
  17.3 1.4 copy.127
  18.7 4.8 %gather_fusion.1 = bf16[48,256,256]{2,1,0:T(8,128)(2,1)} fusion(bf16[256,8,256]{2,0,1:T(8,128)(2,1)S(1)} %copy.125, s32[1024]{0:T(1024)S(1)} %pad_clamp_fusion.1), kind=kCustom, calls=%fused_computation.clone | custom fusion | bytes 12583104 | tf_op jit(solution)/shard_map/jit(_take)/gather | solution.py:82
  23.5 4.9 %gather_fusion.2 = bf16[48,256,256]{2,1,0:T(8,128)(2,1)} fusion(bf16[256,6,256]{2,0,1:T(8,128)(2,1)S(1)} %copy.127, s32[1024]{0:T(1024)S(1)} %pad_clamp_fusion), kind=kCustom, calls=%fused_computation.1.clone | custom fusion | bytes 12583104 | tf_op jit(solution)/shard_map/jit(_take)/gather | solution.py:83
  28.5 9.8 %fusion.17 = bf16[48,256,256]{2,1,0:T(8,128)(2,1)} fusion(bf16[48,256,256]{2,1,0:T(8,128)(2,1)} %gather_fusion.2, pred[48]{0:T(512)(128)(4,1)S(1)} %get-tuple-element.19, bf16[48,256,256]{2,1,0:T(8,128)(2,1)} %gather_fusion.1, pred[48]{0:T(512)(128)(4,1)S(1)} %get-tuple-element.8), kind=kOutput, calls=%fused_computation.21 | convolution fusion | flops 1620049920 | bytes 18874464 | tf_op jit(solution)/shard_map/tsa,tsb->sab/dot_general | solution.py:85
  38.4 13.4 %reshape.265 = bf16[8,256,6,256]{3,2,1,0:T(8,128)(2,1)} reshape(bf16[2048,1536]{1,0:T(8,128)(2,1)} %param.13) | data formatting | bytes 12582912 | tf_op jit(solution)/shard_map/reshape | solution.py:58
  51.8 7.8 %copy.123 = bf16[8,256,6,256]{3,1,2,0:T(8,128)(2,1)} copy(bf16[8,256,6,256]{3,2,1,0:T(8,128)(2,1)} %reshape.265) | data formatting | bytes 12582912 | tf_op jit(solution)/shard_map/reshape | solution.py:58
  59.7 3.5 %gather_fusion = bf16[3,256,256]{2,1,0:T(8,128)(2,1)S(1)} fusion(bf16[8,256,6,256]{3,1,2,0:T(8,128)(2,1)} %copy.123, s32[3]{0:T(128)S(1)} %fusion.149), kind=kCustom, calls=%fused_computation.4 | custom fusion | bytes 786456 | tf_op jit(solution)/shard_map/gather | solution.py:59
  63.2 51.7 %reduce-scatter.3.cloned.1.call-done = bf16[3,256,256]{2,1,0:T(8,128)(2,1)} async-done(((bf16[48,256,256]{2,1,0:T(8,128)(2,1)}), bf16[3,256,256]{2,1,0:T(8,128)(2,1)}) %reduce-scatter.3.cloned.1.call-update) | async-done | bytes 393232 | tf_op jit(solution)/shard_map/reduce_scatter | solution.py:84
  116.0 1.6 multiply_reduce_fusion.3
  119.9 4.9 %gather_fusion.3 = bf16[48,256,256]{2,1,0:T(8,128)(2,1)} fusion(bf16[256,8,256]{2,0,1:T(8,128)(2,1)S(1)} %copy.133, s32[1024]{0:T(1024)S(1)} %pad_clamp_fusion.1), kind=kCustom, calls=%fused_computation.2.clone | custom fusion | bytes 12583104 | tf_op jit(solution)/shard_map/jit(_take)/gather | solution.py:82
  125.4 36.9 %all-gather.2.cloned.1.call-done = bf16[48,256,256]{2,1,0:T(8,128)(2,1)} async-done(((bf16[3,256,256]{2,1,0:T(8,128)(2,1)}), bf16[48,256,256]{2,1,0:T(8,128)(2,1)}) %all-gather.2.cloned.1.call-update) | async-done | bytes 6291472 | tf_op jit(solution)/shard_map/all_gather | solution.py:73
  162.4 9.9 %fusion.14 = bf16[256,48,256]{0,2,1:T(8,128)(2,1)} fusion(bf16[48,256,256]{2,1,0:T(8,128)(2,1)} %all-gather.2.cloned.1.call-done, bf16[48,256,256]{2,1,0:T(8,128)(2,1)} %gather_fusion.3, pred[48]{0:T(512)(128)(4,1)S(1)} %get-tuple-element.8), kind=kOutput, calls=%fused_computation.20 | convolution fusion | flops 1613758464 | bytes 18874416 | tf_op jit(solution)/shard_map/tsa,sab->tsb/dot_general | solution.py:70
  172.3 8.9 %copy.136 = bf16[256,48,256]{2,1,0:T(8,128)(2,1)} copy(bf16[256,48,256]{0,2,1:T(8,128)(2,1)} %fusion.14) | data formatting | bytes 12582912 | tf_op jit(solution)/shard_map/tsa,sab->tsb/transpose | solution.py:70
  181.2 3.7 %fusion.144 = f32[6,256,256]{2,0,1:T(8,128)S(1)} fusion(bf16[256,48,256]{2,1,0:T(8,128)(2,1)} %copy.136, s32[48]{0:T(128)S(1)} %get-tuple-element.20), kind=kOutput, calls=%fused_computation.129 | convolution fusion | flops 37749024 | bytes 7864512 | tf_op jit(solution)/shard_map/tsb,sj->tjb/dot_general | solution.py:76
  185.7 4.9 %gather_fusion.4 = bf16[48,256,256]{2,1,0:T(8,128)(2,1)} fusion(bf16[256,6,256]{2,0,1:T(8,128)(2,1)S(1)} %fusion.55, s32[1024]{0:T(1024)S(1)} %pad_clamp_fusion), kind=kCustom, calls=%fused_computation.3.clone | custom fusion | bytes 12583104 | tf_op jit(solution)/shard_map/jit(_take)/gather | solution.py:83
  190.6 9.7 %fusion.22 = bf16[48,256,256]{2,1,0:T(8,128)(2,1)} fusion(bf16[48,256,256]{2,1,0:T(8,128)(2,1)} %gather_fusion.4, pred[48]{0:T(512)(128)(4,1)S(1)} %get-tuple-element.19, bf16[48,256,256]{2,1,0:T(8,128)(2,1)} %gather_fusion.3, pred[48]{0:T(512)(128)(4,1)S(1)} %get-tuple-element.8), kind=kOutput, calls=%fused_computation.22 | convolution fusion | flops 1620049920 | bytes 18874464 | tf_op jit(solution)/shard_map/tsa,tsb->sab/dot_general | solution.py:85
  202.9 1.3 copy.143
  204.1 70.8 %reduce-scatter.5.cloned.1.call-done = bf16[3,256,256]{2,1,0:T(8,128)(2,1)} async-done(((bf16[48,256,256]{2,1,0:T(8,128)(2,1)}), bf16[3,256,256]{2,1,0:T(8,128)(2,1)}) %reduce-scatter.5.cloned.1.call-update) | async-done | bytes 393232 | tf_op jit(solution)/shard_map/reduce_scatter | solution.py:84
  275.0 1.6 fusion.172
  282.0 1.8 fusion.32
  283.9 2.7 fusion.174
  286.5 5.1 %fusion.29 = bf16[6,256,256]{2,1,0:T(8,128)(2,1)} fusion(f32[6,256,256]{2,1,0:T(8,128)} %fusion.174, f32[256,256]{1,0:T(8,128)S(1)} %fusion.142), kind=kOutput, calls=%fused_computation.25 | convolution fusion | flops 403439616 | bytes 2621440 | tf_op jit(solution)/shard_map/...ij,...jk->...ik/dot_general | solution.py:14
  291.7 1.8 fusion.38
  293.5 2.7 fusion.171
  296.1 5.2 %fusion.35 = bf16[6,256,256]{2,1,0:T(8,128)(2,1)} fusion(f32[6,256,256]{2,1,0:T(8,128)} %fusion.171, f32[256,256]{1,0:T(8,128)S(1)} %fusion.142), kind=kOutput, calls=%fused_computation.29 | convolution fusion | flops 403439616 | bytes 2621440 | tf_op jit(solution)/shard_map/...ij,...jk->...ik/dot_general | solution.py:14
  301.3 4.1 %fusion.103 = bf16[6,256,256]{2,1,0:T(8,128)(2,1)} fusion(bf16[6,256,256]{2,1,0:T(8,128)(2,1)} %bitcast.159, bf16[6,256,256]{2,1,0:T(8,128)(2,1)} %fusion.35, f32[6,256,256]{2,1,0:T(8,128)} %fusion.171, f32[6,256,256]{2,1,0:T(8,128)S(1)} %get-tuple-element.13, f32[6]{0:T(128)S(1)} %power_multiply_fusion.1, f32[256,256]{1,0:T(8,128)S(1)} %fusion.142, ...), kind=kOutput, calls=%fused_computation.87 | convolution fusion | flops 607125504 | bytes 5767198 | tf_op jit(solution)/shard_map/...ij,...jk->...ik/dot_general | solution.py:14
  305.5 1.3 multiply_reduce_fusion.2
  306.8 2.5 multiply_reduce_fusion.1
  309.3 3.1 fusion.98
  312.5 2.1 fusion.140
  (71 shorter events, 15.9 us)
Async XLA Ops:
  7.2 107.7 %reduce-scatter.3.cloned.1.call-start = ((), (), s32[]{:S(2)}) async-start(), calls=%async_computation.2 | async-start | bytes 6684672 | tf_op jit(solution)/shard_map/reduce_scatter | solution.py:84
  38.3 124.0 %all-gather.2.cloned.1.call-start = ((), (), s32[]{:S(2)}) async-start(), calls=%async_computation.3 | async-start | bytes 6684672 | tf_op jit(solution)/shard_map/all_gather | solution.py:73
  38.4 13.4 %copy-start.5 = (bf16[1,3,2,256,256]{4,3,2,1,0:T(8,128)(2,1)S(1)}, bf16[1,3,2,256,256]{4,3,2,1,0:T(8,128)(2,1)}, u32[]{:S(2)}) copy-start(bf16[1,3,2,256,256]{4,3,2,1,0:T(8,128)(2,1)} %param.16) | copy-start | bytes 2359300
  118.6 156.3 %reduce-scatter.5.cloned.1.call-start = ((), (), s32[]{:S(2)}) async-start(), calls=%async_computation.4 | async-start | bytes 6684672 | tf_op jit(solution)/shard_map/reduce_scatter | solution.py:84
  119.9 4.9 %slice-start = ((bf16[2,256,1536]{2,1,0:T(8,128)(2,1)}), bf16[1,256,1536]{2,1,0:T(8,128)(2,1)S(1)}, s32[]{:S(2)}) async-start(bf16[2,256,1536]{2,1,0:T(8,128)(2,1)} %param.12), calls=%async_computation.5 | async-start | bytes 1572864 | tf_op jit(solution)/shard_map/slice | solution.py:78
  200.3 0.7 copy-start.9
  200.3 1.7 copy-start
  274.9 1.6 copy-start.2
  274.9 1.9 copy-start.6
  275.0 1.9 copy-start.8
  279.4 1.0 copy-start.7
  279.6 1.4 copy-start.3
  279.6 1.9 copy-start.4
  305.5 3.9 %copy-start.1 = (f32[6,256,256]{2,1,0:T(8,128)S(1)}, f32[6,256,256]{2,1,0:T(8,128)}, u32[]{:S(2)}) copy-start(f32[6,256,256]{2,1,0:T(8,128)} %fusion.174) | copy-start | bytes 4718596
Sparse Core Ops, SparseCore 0:
  38.4 76.3 reduce-scatter.2
  118.8 43.5 all-gather.1
  200.5 74.4 reduce-scatter.4
where the time goes:
time: 322 us; the launch traced here: 321 us
  waiting for transfers between devices  159 us (49%)
  matrix products  71.7 us (22%)
  local copies, waits for them, and re-layouts  65.4 us (20%)
  between operations  14 us (4%)
  other arithmetic  10.2 us (3%)
    reduce_scatter x2, waiting for transfers between devices, body(): lax.psum_scatter(jnp.einsum('tsa,tsb->sab', left_rows, right_cols, prefer...  123 us
    all_gather x1, waiting for transfers between devices, body(): lax.all_gather(own_weight, 'rep', axis=0, tiled=True)  36.9 us
    dot_general x12, matrix products, exact_dot(): return jnp.einsum('...ij,...jk->...ik', first, second)  29 us
    reshape x2, local copies, waits for them, and re-layouts, body(): grid = weights.reshape(row_blocks, block_size, col_blocks, block_size)  21.2 us
    dot_general x2, matrix products, body(): jnp.einsum('tsa,tsb->sab', left_rows, right_cols, preferred_element_type=...  19.6 us
    dot_general x1, matrix products, body(): jnp.einsum('tsa,sab->tsb', chosen, lax.all_gather(own_weight, 'rep', axis...  9.91 us
    gather x2, local copies, waits for them, and re-layouts, body(): right_cols = jnp.take(dgate_blocks, block_at % col_blocks, axis=1)  9.81 us
    gather x2, local copies, waits for them, and re-layouts, body(): left_rows = jnp.take(feature_blocks, block_at // col_blocks, axis=1)  9.76 us
  transfers between devices with their start and end apart: 3, of which 3 were waited for; matrix products, arithmetic and copies ran while one was open for 11% of the time, Pallas kernels for 0%

commit v1 on v0

--- a/solution.py
+++ b/solution.py
@@ -70,7 +70,10 @@
             products = jnp.einsum(
                 "tsa,sab->tsb",
                 chosen,
-                lax.all_gather(own_weight, "rep", axis=0, tiled=True),
+                jnp.concatenate(
+                    lax.all_to_all(jnp.stack([own_weight] * lax.axis_size("rep")), "rep", 0, 0),
+                    axis=0,
+                ),
                 preferred_element_type=jnp.float32,
             )
             gate_value = jnp.einsum("tsb,sj->tjb", products, column_pick)

time: 322 us -> 372 us (1.16)
  waiting for transfers between devices: 159 us -> 200 us
  starting transfers between devices: 0.3 us -> 4.92 us
    all_to_all x0 -> x1, waiting for transfers between devices: none -> 77.6 us  [body(): lax.all_to_all(jnp.stack([own_weight] * lax.axis_size('rep')), 'rep', 0, 0)]
    all_gather x1 -> x0, waiting for transfers between devices: 36.9 us -> none  [body(): lax.all_gather(own_weight, 'rep', axis=0, tiled=True)]
    all_to_all x0 -> x1, starting transfers between devices: none -> 4.66 us  [body(): lax.all_to_all(jnp.stack([own_weight] * lax.axis_size('rep')), 'rep', 0, 0)]
  transfers between devices with their start and end apart: 3 -> 3, of which waited for: 3 -> 3; matrix products, arithmetic and copies ran while one was open for 11% -> 9% of each run, Pallas kernels for 0% -> 0%
where the time goes in v1:
time: 372 us; the launch traced here: 371 us
  waiting for transfers between devices  200 us (54%)
  matrix products  71.7 us (19%)
  local copies, waits for them, and re-layouts  69 us (19%)
  between operations  14.4 us (4%)
  other arithmetic  10.5 us (3%)
  starting transfers between devices  4.92 us (1%)
    reduce_scatter x2, waiting for transfers between devices, body(): lax.psum_scatter(jnp.einsum('tsa,tsb->sab', left_rows, right_cols, prefer...  122 us
    all_to_all x1, waiting for transfers between devices, body(): lax.all_to_all(jnp.stack([own_weight] * lax.axis_size('rep')), 'rep', 0, 0)  77.6 us
    dot_general x12, matrix products, exact_dot(): return jnp.einsum('...ij,...jk->...ik', first, second)  29 us
    reshape x2, local copies, waits for them, and re-layouts, body(): grid = weights.reshape(row_blocks, block_size, col_blocks, block_size)  21.2 us
    dot_general x2, matrix products, body(): jnp.einsum('tsa,tsb->sab', left_rows, right_cols, preferred_element_type=...  19.6 us
    gather x2, local copies, waits for them, and re-layouts, body(): right_cols = jnp.take(dgate_blocks, block_at % col_blocks, axis=1)  9.81 us
    gather x2, local copies, waits for them, and re-layouts, body(): left_rows = jnp.take(feature_blocks, block_at // col_blocks, axis=1)  9.76 us
    dot_general x1, matrix products, body(): jnp.einsum('tsa,sab->tsb', chosen, jnp.concatenate(lax.all_to_all(jnp.sta...  9.14 us
  transfers between devices with their start and end apart: 3, of which 3 were waited for; matrix products, arithmetic and copies ran while one was open for 9% of the time, Pallas kernels for 0%

profile of v1, /device:TPU:32, one launch (start us, length us, event | category | flops | bytes accessed | tf_op | source)
XLA Modules:
  0.0 370.6 jit_solution(13101057634628385193)
XLA Ops:
  8.0 1.7 fusion.168
  10.8 5.4 %fusion.46 = bf16[256,1536]{1,0:T(8,128)(2,1)S(1)} fusion(bf16[2048,1536]{1,0:T(8,128)(2,1)} %param.13, bf16[2,256,1536]{2,1,0:T(8,128)(2,1)} %param.12, bf16[2,256,2048]{2,1,0:T(8,128)(2,1)} %param.11), kind=kOutput, calls=%fused_computation.43 | convolution fusion | flops 1614544896 | bytes 8912896 | tf_op jit(solution)/shard_map/dot_general | solution.py:67
  17.3 1.4 copy.127
  18.7 4.8 %gather_fusion.1 = bf16[48,256,256]{2,1,0:T(8,128)(2,1)} fusion(bf16[256,8,256]{2,0,1:T(8,128)(2,1)S(1)} %copy.125, s32[1024]{0:T(1024)S(1)} %pad_clamp_fusion.1), kind=kCustom, calls=%fused_computation.clone | custom fusion | bytes 12583104 | tf_op jit(solution)/shard_map/jit(_take)/gather | solution.py:85
  23.5 4.9 %gather_fusion.2 = bf16[48,256,256]{2,1,0:T(8,128)(2,1)} fusion(bf16[256,6,256]{2,0,1:T(8,128)(2,1)S(1)} %copy.127, s32[1024]{0:T(1024)S(1)} %pad_clamp_fusion), kind=kCustom, calls=%fused_computation.1.clone | custom fusion | bytes 12583104 | tf_op jit(solution)/shard_map/jit(_take)/gather | solution.py:86
  28.5 9.8 %fusion.17 = bf16[48,256,256]{2,1,0:T(8,128)(2,1)} fusion(bf16[48,256,256]{2,1,0:T(8,128)(2,1)} %gather_fusion.2, pred[48]{0:T(512)(128)(4,1)S(1)} %get-tuple-element.19, bf16[48,256,256]{2,1,0:T(8,128)(2,1)} %gather_fusion.1, pred[48]{0:T(512)(128)(4,1)S(1)} %get-tuple-element.8), kind=kOutput, calls=%fused_computation.21 | convolution fusion | flops 1620049920 | bytes 18874464 | tf_op jit(solution)/shard_map/tsa,tsb->sab/dot_general | solution.py:88
  38.3 13.4 %reshape.271 = bf16[8,256,6,256]{3,2,1,0:T(8,128)(2,1)} reshape(bf16[2048,1536]{1,0:T(8,128)(2,1)} %param.13) | data formatting | bytes 12582912 | tf_op jit(solution)/shard_map/reshape | solution.py:58
  51.7 7.8 %copy.123 = bf16[8,256,6,256]{3,1,2,0:T(8,128)(2,1)} copy(bf16[8,256,6,256]{3,2,1,0:T(8,128)(2,1)} %reshape.271) | data formatting | bytes 12582912 | tf_op jit(solution)/shard_map/reshape | solution.py:58
  59.7 3.5 gather_fusion
  63.1 51.7 %reduce-scatter.3.cloned.1.call-done = bf16[3,256,256]{2,1,0:T(8,128)(2,1)} async-done(((bf16[48,256,256]{2,1,0:T(8,128)(2,1)}), bf16[3,256,256]{2,1,0:T(8,128)(2,1)}) %reduce-scatter.3.cloned.1.call-update) | async-done | bytes 393232 | tf_op jit(solution)/shard_map/reduce_scatter | solution.py:87
  116.0 2.4 multiply_reduce_fusion.3
  119.9 3.4 stack.49
  123.3 4.7 %all-to-all-start = ((bf16[16,3,256,256]{2,3,1,0:T(8,128)(2,1)}), bf16[16,3,256,256]{2,3,1,0:T(8,128)(2,1)}, u32[]{:S(2)}, u32[]{:S(2)}) async-start(bf16[16,3,256,256]{2,3,1,0:T(8,128)(2,1)} %stack.49), calls=%async_computation.1 | async-start | bytes 12582912 | tf_op jit(solution)/shard_map/all_to_all | solution.py:74
  129.3 4.9 %gather_fusion.3 = bf16[48,256,256]{2,1,0:T(8,128)(2,1)} fusion(bf16[256,8,256]{2,0,1:T(8,128)(2,1)S(1)} %copy.133, s32[1024]{0:T(1024)S(1)} %pad_clamp_fusion.1), kind=kCustom, calls=%fused_computation.2.clone | custom fusion | bytes 12583104 | tf_op jit(solution)/shard_map/jit(_take)/gather | solution.py:85
  134.7 77.6 %all-to-all-done = bf16[16,3,256,256]{2,3,1,0:T(8,128)(2,1)} async-done(((bf16[16,3,256,256]{2,3,1,0:T(8,128)(2,1)}), bf16[16,3,256,256]{2,3,1,0:T(8,128)(2,1)}, u32[]{:S(2)}, u32[]{:S(2)}) %all-to-all-start) | async-done | bytes 6291488 | tf_op jit(solution)/shard_map/all_to_all | solution.py:74
  212.4 9.1 %fusion.14 = bf16[256,48,256]{0,2,1:T(8,128)(2,1)} fusion(bf16[48,256,256]{1,2,0:T(8,128)(2,1)} %bitcast.14, bf16[48,256,256]{2,1,0:T(8,128)(2,1)} %gather_fusion.3, pred[48]{0:T(512)(128)(4,1)S(1)} %get-tuple-element.8), kind=kOutput, calls=%fused_computation.20 | convolution fusion | flops 1613758464 | bytes 18874416 | tf_op jit(solution)/shard_map/tsa,sab->tsb/dot_general | solution.py:70
  221.5 8.9 %copy.136 = bf16[256,48,256]{2,1,0:T(8,128)(2,1)} copy(bf16[256,48,256]{0,2,1:T(8,128)(2,1)} %fusion.14) | data formatting | bytes 12582912 | tf_op jit(solution)/shard_map/tsa,sab->tsb/transpose | solution.py:70
  230.4 3.7 fusion.144
  234.9 4.9 %gather_fusion.4 = bf16[48,256,256]{2,1,0:T(8,128)(2,1)} fusion(bf16[256,6,256]{2,0,1:T(8,128)(2,1)S(1)} %fusion.55, s32[1024]{0:T(1024)S(1)} %pad_clamp_fusion), kind=kCustom, calls=%fused_computation.3.clone | custom fusion | bytes 12583104 | tf_op jit(solution)/shard_map/jit(_take)/gather | solution.py:86
  239.8 9.7 %fusion.22 = bf16[48,256,256]{2,1,0:T(8,128)(2,1)} fusion(bf16[48,256,256]{2,1,0:T(8,128)(2,1)} %gather_fusion.4, pred[48]{0:T(512)(128)(4,1)S(1)} %get-tuple-element.19, bf16[48,256,256]{2,1,0:T(8,128)(2,1)} %gather_fusion.3, pred[48]{0:T(512)(128)(4,1)S(1)} %get-tuple-element.8), kind=kOutput, calls=%fused_computation.22 | convolution fusion | flops 1620049920 | bytes 18874464 | tf_op jit(solution)/shard_map/tsa,tsb->sab/dot_general | solution.py:88
  253.3 70.8 %reduce-scatter.5.cloned.1.call-done = bf16[3,256,256]{2,1,0:T(8,128)(2,1)} async-done(((bf16[48,256,256]{2,1,0:T(8,128)(2,1)}), bf16[3,256,256]{2,1,0:T(8,128)(2,1)}) %reduce-scatter.5.cloned.1.call-update) | async-done | bytes 393232 | tf_op jit(solution)/shard_map/reduce_scatter | solution.py:87
  324.1 1.6 fusion.172
  331.2 1.8 fusion.32
  333.0 2.7 fusion.174
  335.7 5.1 %fusion.29 = bf16[6,256,256]{2,1,0:T(8,128)(2,1)} fusion(f32[6,256,256]{2,1,0:T(8,128)} %fusion.174, f32[256,256]{1,0:T(8,128)S(1)} %fusion.142), kind=kOutput, calls=%fused_computation.25 | convolution fusion | flops 403439616 | bytes 2621440 | tf_op jit(solution)/shard_map/...ij,...jk->...ik/dot_general | solution.py:14
  340.8 1.8 fusion.38
  342.6 2.7 fusion.171
  345.3 5.2 %fusion.35 = bf16[6,256,256]{2,1,0:T(8,128)(2,1)} fusion(f32[6,256,256]{2,1,0:T(8,128)} %fusion.171, f32[256,256]{1,0:T(8,128)S(1)} %fusion.142), kind=kOutput, calls=%fused_computation.29 | convolution fusion | flops 403439616 | bytes 2621440 | tf_op jit(solution)/shard_map/...ij,...jk->...ik/dot_general | solution.py:14
  350.5 4.1 %fusion.103 = bf16[6,256,256]{2,1,0:T(8,128)(2,1)} fusion(bf16[6,256,256]{2,1,0:T(8,128)(2,1)} %bitcast.160, bf16[6,256,256]{2,1,0:T(8,128)(2,1)} %fusion.35, f32[6,256,256]{2,1,0:T(8,128)} %fusion.171, f32[6,256,256]{2,1,0:T(8,128)S(1)} %get-tuple-element.13, f32[6]{0:T(128)S(1)} %power_multiply_fusion.1, f32[256,256]{1,0:T(8,128)S(1)} %fusion.142, ...), kind=kOutput, calls=%fused_computation.87 | convolution fusion | flops 607125504 | bytes 5767198 | tf_op jit(solution)/shard_map/...ij,...jk->...ik/dot_general | solution.py:14
  355.9 2.5 multiply_reduce_fusion.1
  358.5 3.1 fusion.98
  361.6 2.1 fusion.140
  (74 shorter events, 19.0 us)
Async XLA Ops:
  7.2 107.6 %reduce-scatter.3.cloned.1.call-start = ((), (), s32[]{:S(2)}) async-start(), calls=%async_computation.3 | async-start | bytes 6684672 | tf_op jit(solution)/shard_map/reduce_scatter | solution.py:87
  38.3 13.4 %copy-start.6 = (bf16[1,3,2,256,256]{4,3,2,1,0:T(8,128)(2,1)S(1)}, bf16[1,3,2,256,256]{4,3,2,1,0:T(8,128)(2,1)}, u32[]{:S(2)}) copy-start(bf16[1,3,2,256,256]{4,3,2,1,0:T(8,128)(2,1)} %param.16) | copy-start | bytes 2359300
  119.7 3.5 copy-start.5
  123.3 89.1 %all-to-all-start = ((bf16[16,3,256,256]{2,3,1,0:T(8,128)(2,1)}), bf16[16,3,256,256]{2,3,1,0:T(8,128)(2,1)}, u32[]{:S(2)}, u32[]{:S(2)}) async-start(bf16[16,3,256,256]{2,3,1,0:T(8,128)(2,1)} %stack.49), calls=%async_computation.1 | async-start | bytes 12582912 | tf_op jit(solution)/shard_map/all_to_all | solution.py:74
  128.0 196.1 %reduce-scatter.5.cloned.1.call-start = ((), (), s32[]{:S(2)}) async-start(), calls=%async_computation.4 | async-start | bytes 6684672 | tf_op jit(solution)/shard_map/reduce_scatter | solution.py:87
  129.2 4.9 %slice-start = ((bf16[2,256,1536]{2,1,0:T(8,128)(2,1)}), bf16[1,256,1536]{2,1,0:T(8,128)(2,1)S(1)}, s32[]{:S(2)}) async-start(bf16[2,256,1536]{2,1,0:T(8,128)(2,1)} %param.12), calls=%async_computation.5 | async-start | bytes 1572864 | tf_op jit(solution)/shard_map/slice | solution.py:81
  249.6 0.7 copy-start.10
  249.6 1.7 copy-start
  324.1 1.6 copy-start.2
  324.1 1.9 copy-start.7
  324.1 1.9 copy-start.9
  328.6 1.0 copy-start.8
  328.8 1.4 copy-start.3
  328.8 1.9 copy-start.4
  354.6 3.9 %copy-start.1 = (f32[6,256,256]{2,1,0:T(8,128)S(1)}, f32[6,256,256]{2,1,0:T(8,128)}, u32[]{:S(2)}) copy-start(f32[6,256,256]{2,1,0:T(8,128)} %fusion.174) | copy-start | bytes 4718596
Sparse Core Ops, SparseCore 0:
  38.4 76.3 reduce-scatter.2
  249.7 74.3 reduce-scatter.4
